TPU v7x, 32 devices: a whole 2x2x4 slice. The times are simulated.
32 devices in a mesh: groups: 2 (over x), seq: 16 (over z, y, core).
Axes of the slice: x: 2, y: 2, z: 4, core: 2. Of those that a mesh axis runs over, the one named last changes fastest.
Arguments:
- attn_query: bfloat16 [8192, 2048], P(('groups', 'seq')), parts along dimension 0, may hold values from -16 to 16
- attn_key: bfloat16 [8192, 2048], P(('groups', 'seq')), parts along dimension 0, may hold values from -16 to 16
- attn_value: bfloat16 [8192, 2048], P(('groups', 'seq')), parts along dimension 0, may hold values from -6 to 6
- mesa_query: bfloat16 [8192, 2048], P(('groups', 'seq')), parts along dimension 0, may hold values from -6 to 6
- mesa_key: bfloat16 [8192, 2048], P(('groups', 'seq')), parts along dimension 0, may hold values from -16 to 16
- log_decay: float32 [8192, 16], P(('groups', 'seq')), parts along dimension 0, may hold values from -1 to 0
- input_gate: float32 [8192, 16], P(('groups', 'seq')), parts along dimension 0, may hold values from 0.2 to 1
- regularizer: float32 [16, 128], replicated, may hold values from 0.5 to 4
Outputs:
- attention: bfloat16 [8192, 2048], P(('groups', 'seq')), parts along dimension 0
- mesa_out: bfloat16 [8192, 2048], P(('groups', 'seq')), parts along dimension 0
There are 2 independent parts, one for each index of `groups`. A program takes and returns all parts, laid end to end along the dimension named above; an argument that names none is the same for every part. Nothing has to cross between parts.
All inputs are finite; a program needn't handle non-finite values.
Results may differ from a plain program's by a relative error of at most 0.017.
Values may be sent and summed in bfloat16 or wider, within the bound.
No kernel may reach another device: no remote copies, remote signals or barrier semaphores. Data moves between devices by JAX's collectives and lax.ppermute only.
A program may use at most 128 MiB of HBM per device.

v0:
```python
import jax
import jax.numpy as jnp
from jax import lax
from jax.sharding import PartitionSpec as P

WINDOW = 2048
SPAN = 64
CG_ITERS = 8


exact_mode = lax.Precision.HIGHEST
masked_score = -1e30


def prefix(shard, axis, join, neutral):
    place = lax.axis_index(axis)
    gathered = jax.tree.map(
        lambda a, kind: lax.all_gather(a.astype(kind), axis), shard, (jnp.bfloat16, jnp.bfloat16)
    )
    state = jax.tree.map(lambda a, e: jnp.zeros_like(a) + jnp.asarray(e, a.dtype), shard, neutral)

    def one(lap, state):
        return join(
            state,
            jax.tree.map(
                lambda a, own: lax.dynamic_index_in_dim(a, lap, 0, False).astype(own.dtype),
                gathered,
                shard,
            ),
        )

    return lax.fori_loop(0, place, one, state)


def passed_along(value, axis, steps):
    count = lax.axis_size(axis)
    first, last = (max(0, -steps), min(count, count - steps))
    return lax.ppermute(value, axis, [(source, source + steps) for source in range(first, last)])


def span_update(states, inputs, ridge_diag):
    gram_start, cross_start = states
    queries, key_rows, value_rows, log_rates, gate_rows = inputs
    q_heads = jnp.transpose(queries, (1, 0, 2))
    k_heads = jnp.transpose(key_rows, (1, 0, 2))
    v_heads = jnp.transpose(value_rows, (1, 0, 2))
    cumulative = jnp.transpose(jnp.cumsum(log_rates, axis=0))
    length = cumulative.shape[1]
    causal = (jnp.arange(length)[:, None] >= jnp.arange(length)[None, :])[None]
    distance = cumulative[:, :, None] - cumulative[:, None, :]
    decay_mix = (
        jnp.where(causal, jnp.exp(jnp.where(causal, distance, 0.0)), 0.0)
        * jnp.transpose(gate_rows)[:, None, :]
    )
    start_scale = jnp.exp(cumulative)[:, :, None]
    iterate = jnp.zeros_like(q_heads)
    remain = q_heads
    search = q_heads
    norm_now = jnp.sum(remain * remain, axis=-1, keepdims=True)
    for sweep_index in range(CG_ITERS):
        carried = start_scale * jnp.einsum("hcd,hed->hce", search, gram_start, precision=exact_mode)
        operator_products = jnp.einsum("hjd,hid->hji", search, k_heads, precision=exact_mode)
        local_part = jnp.einsum(
            "hji,hid->hjd", decay_mix * operator_products, k_heads, precision=exact_mode
        )
        image_vec = carried + local_part + ridge_diag[:, None, :] * search
        step_size = norm_now / (jnp.sum(search * image_vec, axis=-1, keepdims=True) + 1e-06)
        iterate = iterate + step_size * search
        remain = remain - step_size * image_vec
        norm_next = jnp.sum(remain * remain, axis=-1, keepdims=True)
        search = remain + norm_next / (norm_now + 1e-06) * search
        norm_now = norm_next
    products = jnp.einsum("hjd,hid->hji", iterate, k_heads, precision=exact_mode)
    mesa_rows = start_scale * jnp.einsum("hje,hde->hjd", iterate, cross_start, precision=exact_mode)
    mesa_rows = mesa_rows + jnp.einsum(
        "hji,hid->hjd", decay_mix * products, v_heads, precision=exact_mode
    )
    tail_weight = (jnp.exp(cumulative[:, -1:] - cumulative) * jnp.transpose(gate_rows))[:, :, None]
    end_scale = jnp.exp(cumulative[:, -1])[:, None, None]
    gram_end = end_scale * gram_start + jnp.einsum(
        "hid,hie->hde", k_heads * tail_weight, k_heads, precision=exact_mode
    )
    cross_end = end_scale * cross_start + jnp.einsum(
        "hid,hie->hde", v_heads * tail_weight, k_heads, precision=exact_mode
    )
    return ((gram_end, cross_end), jnp.transpose(mesa_rows, (1, 0, 2)))


def mesa_pass(
    queries, key_rows, value_rows, log_rates, gate_rows, ridge_diag, gram_start, cross_start
):
    row_total = queries.shape[0]
    span_count = row_total // SPAN

    def shaped(array_in):
        return array_in.reshape((span_count, SPAN) + array_in.shape[1:])

    def advance(states, inputs):
        return span_update(states, inputs, ridge_diag)

    finished, outputs = lax.scan(
        advance,
        (gram_start, cross_start),
        (
            shaped(queries),
            shaped(key_rows),
            shaped(value_rows),
            shaped(log_rates),
            shaped(gate_rows),
        ),
    )
    return outputs.reshape(row_total, -1)


def fold_block(state_now, queries, key_value, query_first, key_first):
    running_max, running_sum, weighted = state_now
    row_count, head_count, head_size = queries.shape
    key_rows = key_value[0].reshape(-1, head_count, head_size)
    value_rows = key_value[1].reshape(-1, head_count, head_size)
    scores = jnp.einsum(
        "qhd,khd->hqk", queries, key_rows, preferred_element_type=jnp.float32
    ) * head_size ** (-0.5)
    query_pos = query_first + jnp.arange(row_count, dtype=jnp.int32)[:, None]
    key_pos = key_first + jnp.arange(key_rows.shape[0], dtype=jnp.int32)[None, :]
    distance = query_pos - key_pos
    inside = ((distance >= 0) & (distance < WINDOW) & (key_pos >= 0))[None]
    scores = jnp.where(inside, scores, masked_score)
    new_max = jnp.maximum(running_max, jnp.max(scores, axis=-1))
    weights = jnp.exp(scores - new_max[:, :, None]) * inside.astype(jnp.float32)
    rescale = jnp.exp(running_max - new_max)
    running_sum = running_sum * rescale + jnp.sum(weights, axis=-1)
    weighted = weighted * rescale[:, :, None] + jnp.einsum(
        "hqk,khd->hqd", weights.astype(jnp.bfloat16), value_rows, preferred_element_type=jnp.float32
    )
    return (new_max, running_sum, weighted)


def combine_pair(earlier, later):
    return (earlier[0] + later[0], jnp.exp(later[0])[:, None, None] * earlier[1] + later[1])


def body(
    attn_query, attn_key, attn_value, mesa_query, mesa_key, log_decay, input_gate, regularizer
):
    row_count = attn_query.shape[0]
    head_count, head_size = regularizer.shape
    shape3 = (row_count, head_count, head_size)
    slab_first = lax.axis_index("seq") * row_count
    keys_float = mesa_key.astype(jnp.float32).reshape(shape3)
    slab_log = jnp.sum(log_decay, axis=0)
    tail_log = slab_log[None, :] - jnp.cumsum(log_decay, axis=0)
    weight_rows = (jnp.exp(tail_log) * input_gate)[:, :, None]
    gram_local = jnp.einsum(
        "lhd,lhe->hde", keys_float * weight_rows, keys_float, precision=exact_mode
    )
    zero_log = jnp.zeros_like(slab_log)
    zero_state = jnp.zeros_like(gram_local)
    gram_prefix = prefix((slab_log, gram_local), "seq", combine_pair, (zero_log, zero_state))[1]
    queries = attn_query.reshape(shape3)
    key_value = jnp.stack([attn_key, attn_value])
    state_now = (
        jnp.full((head_count, row_count), masked_score, jnp.float32),
        jnp.zeros((head_count, row_count), jnp.float32),
        jnp.zeros((head_count, row_count, head_size), jnp.float32),
    )
    state_now = fold_block(state_now, queries, key_value, slab_first, slab_first)
    reach = -(-WINDOW // row_count)
    moving = key_value
    for hop_index in range(1, reach + 1):
        moving = passed_along(moving, "seq", 1)
        state_now = fold_block(
            state_now, queries, moving, slab_first, slab_first - hop_index * row_count
        )
    normed = state_now[2] / state_now[1][:, :, None]
    attention = jnp.transpose(normed, (1, 0, 2)).reshape(row_count, -1).astype(jnp.bfloat16)
    values_float = attention.astype(jnp.float32).reshape(shape3)
    cross_local = jnp.einsum(
        "lhd,lhe->hde", values_float * weight_rows, keys_float, precision=exact_mode
    )
    cross_prefix = prefix((slab_log, cross_local), "seq", combine_pair, (zero_log, zero_state))[1]
    mesa_out = mesa_pass(
        mesa_query.astype(jnp.float32).reshape(shape3),
        keys_float,
        values_float,
        log_decay,
        input_gate,
        regularizer,
        gram_prefix,
        cross_prefix,
    )
    return (attention, mesa_out.astype(jnp.bfloat16))


def solution(mesh):
    return jax.shard_map(
        body,
        mesh=mesh,
        in_specs=(
            P(("groups", "seq"), None),
            P(("groups", "seq"), None),
            P(("groups", "seq"), None),
            P(("groups", "seq"), None),
            P(("groups", "seq"), None),
            P(("groups", "seq"), None),
            P(("groups", "seq"), None),
            P(),
        ),
        out_specs=(P(("groups", "seq"), None), P(("groups", "seq"), None)),
        check_vma=False,
    )
```

profile of v0, /device:TPU:29, one launch (start us, length us, event | category | flops | bytes accessed | tf_op | source)
XLA Modules:
  0.0 676.4 jit_solution(13662638637842191389)
XLA Ops:
  13.9 4.9 collective-permute-done
  21.4 26.1 %collective-permute-done.1 = bf16[2,256,2048]{1,2,0:T(8,128)(2,1)S(1)} collective-permute-done((bf16[2,256,2048]{1,2,0:T(8,128)(2,1)S(1)}, bf16[2,256,2048]{1,2,0:T(8,128)(2,1)S(1)}, u32[]{:S(2)}, u32[]{:S(2)}) %collective-permute-start.1) | collective-permute-done | bytes 2097184 | tf_op jit(solution)/shard_map/ppermute | solution.py:38
  50.1 26.2 %collective-permute-done.2 = bf16[2,256,2048]{1,2,0:T(8,128)(2,1)} collective-permute-done((bf16[2,256,2048]{1,2,0:T(8,128)(2,1)S(1)}, bf16[2,256,2048]{1,2,0:T(8,128)(2,1)}, u32[]{:S(2)}, u32[]{:S(2)}) %collective-permute-start.2) | collective-permute-done | bytes 2097184 | tf_op jit(solution)/shard_map/ppermute | solution.py:38
  83.6 5.0 fusion.161
  88.7 15.2 %collective-permute-done.3 = bf16[2,256,2048]{1,2,0:T(8,128)(2,1)} collective-permute-done((bf16[2,256,2048]{1,2,0:T(8,128)(2,1)}, bf16[2,256,2048]{1,2,0:T(8,128)(2,1)}, u32[]{:S(2)}, u32[]{:S(2)}) %collective-permute-start.3) | collective-permute-done | bytes 2097184 | tf_op jit(solution)/shard_map/ppermute | solution.py:38
  108.2 24.6 %collective-permute-done.4 = bf16[2,256,2048]{1,2,0:T(8,128)(2,1)} collective-permute-done((bf16[2,256,2048]{1,2,0:T(8,128)(2,1)}, bf16[2,256,2048]{1,2,0:T(8,128)(2,1)}, u32[]{:S(2)}, u32[]{:S(2)}) %collective-permute-start.4) | collective-permute-done | bytes 2097184 | tf_op jit(solution)/shard_map/ppermute | solution.py:38
  141.7 20.7 %collective-permute-done.5 = bf16[2,256,2048]{1,2,0:T(8,128)(2,1)S(1)} collective-permute-done((bf16[2,256,2048]{1,2,0:T(8,128)(2,1)}, bf16[2,256,2048]{1,2,0:T(8,128)(2,1)S(1)}, u32[]{:S(2)}, u32[]{:S(2)}) %collective-permute-start.5) | collective-permute-done | bytes 2097184 | tf_op jit(solution)/shard_map/ppermute | solution.py:38
  174.4 30.7 %collective-permute-done.6 = bf16[2,256,2048]{1,2,0:T(8,128)(2,1)S(1)} collective-permute-done((bf16[2,256,2048]{1,2,0:T(8,128)(2,1)S(1)}, bf16[2,256,2048]{1,2,0:T(8,128)(2,1)S(1)}, u32[]{:S(2)}, u32[]{:S(2)}) %collective-permute-start.6) | collective-permute-done | bytes 2097184 | tf_op jit(solution)/shard_map/ppermute | solution.py:38
  211.7 29.0 %collective-permute-done.7 = bf16[2,256,2048]{1,2,0:T(8,128)(2,1)S(1)} collective-permute-done((bf16[2,256,2048]{1,2,0:T(8,128)(2,1)S(1)}, bf16[2,256,2048]{1,2,0:T(8,128)(2,1)S(1)}, u32[]{:S(2)}, u32[]{:S(2)}) %collective-permute-start.7) | collective-permute-done | bytes 2097184 | tf_op jit(solution)/shard_map/ppermute | solution.py:38
  257.8 4.3 fusion.96
  273.5 7.3 %fusion.104 = bf16[256,16,128]{2,0,1:T(8,128)(2,1)S(1)} fusion(f32[16,256,128]{2,1,0:T(8,128)S(1)} %fusion.86, f32[16,256,128]{2,1,0:T(8,128)S(1)} %fusion.88, f32[16,256,128]{2,1,0:T(8,128)S(1)} %fusion.90, f32[16,256,128]{2,1,0:T(8,128)S(1)} %fusion.92, f32[16,256,128]{2,1,0:T(8,128)S(1)} %fusion.94, f32[16,256,128]{2,1,0:T(8,128)S(1)} %copy-done.95, ...), kind=kOutput, calls=%fused_computation.196 | convolution fusion | flops 283639808 | bytes 23576576 | tf_op jit(solution)/shard_map/hqk,khd->hqd/dot_general | solution.py:132
  289.4 68.2 %all-reduce = bf16[256]{0:T(256)(128)(2,1)S(1)} all-reduce(bf16[256]{0:T(256)(128)(2,1)S(1)} %dynamic-update-slice), channel_id=2, replica_groups=mesh['groups'=2,'seq'=16] {'seq'}, use_global_device_ids=true, to_apply=%add | all-reduce | flops 256 | bytes 1024
  363.3 20.3 %while.38 = (s32[]{:T(128)}, f32[16,128,128]{2,1,0:T(8,128)S(1)}, s32[]{:T(128)}, bf16[16,16]{1,0:T(8,128)(2,1)S(1)}, bf16[16,16,128,128]{3,2,1,0:T(8,128)(2,1)}, /*index=5*/s32[]{:T(128)}, s32[]{:T(128)}, s32[]{:T(128)}) while((s32[]{:T(128)}, f32[16,128,128]{2,1,0:T(8,128)S(1)}, s32[]{:T(128)}, bf16[16,16]{1,0:T(8,128)(2,1)S(1)}, ...), condition=%wide.region_22.23_spmd, body=%wide.region_21.22_spmd.sunk | while | flops 786453 | bytes 2621727 | solution.py:32
  390.9 13.0 %all-gather.8.cloned.1.call-done = bf16[256,128,128]{2,1,0:T(8,128)(2,1)} async-done(((bf16[16,128,128]{2,1,0:T(8,128)(2,1)}), bf16[256,128,128]{2,1,0:T(8,128)(2,1)}) %all-gather.8.cloned.1.call-update) | async-done | bytes 8388624 | tf_op jit(solution)/shard_map/all_gather | solution.py:18
  405.0 37.7 %while.39 = (s32[]{:T(128)}, f32[16,128,128]{2,1,0:T(8,128)}, s32[]{:T(128)}, bf16[16,16]{1,0:T(8,128)(2,1)S(1)}, bf16[16,16,128,128]{3,2,1,0:T(8,128)(2,1)}, /*index=5*/s32[]{:T(128)}, s32[]{:T(128)}, s32[]{:T(128)}) while((s32[]{:T(128)}, f32[16,128,128]{2,1,0:T(8,128)}, s32[]{:T(128)}, bf16[16,16]{1,0:T(8,128)(2,1)S(1)}, ...), condition=%wide.region_24.25_spmd, body=%wide.region_23.24_spmd.sunk | while | flops 786453 | bytes 2621727 | solution.py:32
  442.7 223.3 %while.40 = (s32[]{:T(128)}, f32[16,128,128]{2,1,0:T(8,128)S(1)}, f32[16,128,128]{2,1,0:T(8,128)}, bf16[4,64,16,128]{3,1,2,0:T(8,128)(2,1)}, f32[4,64,16]{2,1,0:...) while((s32[]{:T(128)}, f32[16,128,128]{2,1,0:T(8,128)S(1)}, ...), condition=%wide.region_43.44_spmd, body=%wide.region_25.43_spmd.sunk | while | flops 4045949952 | bytes 85774864 | solution.py:101
  487.1 4.4 fusion.472
  493.6 4.4 convolution_add_fusion.5
  542.5 4.4 fusion.472
  549.0 4.4 convolution_add_fusion.5
  598.0 4.4 fusion.472
  604.5 4.4 convolution_add_fusion.5
  653.3 4.4 fusion.472
  659.9 4.4 convolution_add_fusion.5
  (627 shorter events, 344.4 us)
Async XLA Ops:
  7.2 126.9 %copy-start = (bf16[256,2048]{1,0:T(8,128)(2,1)S(1)}, bf16[256,2048]{1,0:T(8,128)(2,1)}, u32[]{:S(2)}) copy-start(bf16[256,2048]{1,0:T(8,128)(2,1)} %param.14) | copy-start | bytes 3145732
  7.2 70.4 %copy-start.56 = (f32[256,16]{0,1:T(8,128)S(1)}, f32[256,16]{0,1:T(8,128)}, u32[]{:S(2)}) copy-start(f32[256,16]{0,1:T(8,128)} %param.19) | copy-start | bytes 49156
  7.2 71.3 %copy-start.4 = (bf16[256,2048]{1,0:T(8,128)(2,1)S(1)}, bf16[256,2048]{1,0:T(8,128)(2,1)}, u32[]{:S(2)}) copy-start(bf16[256,2048]{1,0:T(8,128)(2,1)} %param.18) | copy-start | bytes 3145732
  7.2 355.9 %all-gather.6.cloned.1.call-start = ((), (), s32[]{:S(2)}) async-start(), calls=%async_computation | async-start | bytes 8912896 | tf_op jit(solution)/shard_map/all_gather | solution.py:18
  12.6 6.2 collective-permute-start
  20.1 27.3 %collective-permute-start.1 = (bf16[2,256,2048]{1,2,0:T(8,128)(2,1)S(1)}, bf16[2,256,2048]{1,2,0:T(8,128)(2,1)S(1)}, u32[]{:S(2)}, u32[]{:S(2)}) collective-permute-start(bf16[2,256,2048]{1,2,0:T(8,128)(2,1)S(1)} %collective-permute-done), channel_id=1, source_target_pairs={{0,1},{1,2},{2,3},{3,4},{4,5},{5,6},{6,7},{7,8},{8,9},{9,10},{10,1... | collective-permute-start | bytes 6291464 | tf_op jit(solution)/shard_map/ppermute | solution.py:38
  48.8 27.5 %collective-permute-start.2 = (bf16[2,256,2048]{1,2,0:T(8,128)(2,1)S(1)}, bf16[2,256,2048]{1,2,0:T(8,128)(2,1)}, u32[]{:S(2)}, u32[]{:S(2)}) collective-permute-start(bf16[2,256,2048]{1,2,0:T(8,128)(2,1)S(1)} %collective-permute-done.1), channel_id=1, source_target_pairs={{0,1},{1,2},{2,3},{3,4},{4,5},{5,6},{6,7},{7,8},{8,9},{9,10},{10,1... | collective-permute-start | bytes 6291464 | tf_op jit(solution)/shard_map/ppermute | solution.py:38
  76.3 27.7 %collective-permute-start.3 = (bf16[2,256,2048]{1,2,0:T(8,128)(2,1)}, bf16[2,256,2048]{1,2,0:T(8,128)(2,1)}, u32[]{:S(2)}, u32[]{:S(2)}) collective-permute-start(bf16[2,256,2048]{1,2,0:T(8,128)(2,1)} %collective-permute-done.2), channel_id=1, source_target_pairs={{0,1},{1,2},{2,3},{3,4},{4,5},{5,6},{6,7},{7,8},{8,9},{9,10},{10,1... | collective-permute-start | bytes 6291464 | tf_op jit(solution)/shard_map/ppermute | solution.py:38
  83.6 52.6 %copy-start.60 = (f32[256,16]{0,1:T(8,128)}, f32[256,16]{0,1:T(8,128)S(1)}, u32[]{:S(2)}) copy-start(f32[256,16]{0,1:T(8,128)S(1)} %fusion.228) | copy-start | bytes 49156
  88.7 315.2 %all-gather.8.cloned.1.call-start = ((), (), s32[]{:S(2)}) async-start(), calls=%async_computation.1 | async-start | bytes 8912896 | tf_op jit(solution)/shard_map/all_gather | solution.py:18
  103.9 28.9 %collective-permute-start.4 = (bf16[2,256,2048]{1,2,0:T(8,128)(2,1)}, bf16[2,256,2048]{1,2,0:T(8,128)(2,1)}, u32[]{:S(2)}, u32[]{:S(2)}) collective-permute-start(bf16[2,256,2048]{1,2,0:T(8,128)(2,1)} %collective-permute-done.3), channel_id=1, source_target_pairs={{0,1},{1,2},{2,3},{3,4},{4,5},{5,6},{6,7},{7,8},{8,9},{9,10},{10,1... | collective-permute-start | bytes 6291464 | tf_op jit(solution)/shard_map/ppermute | solution.py:38
  105.5 30.8 %copy-start.9 = (bf16[2,256,2048]{1,2,0:T(8,128)(2,1)S(1)}, bf16[2,256,2048]{1,2,0:T(8,128)(2,1)}, u32[]{:S(2)}) copy-start(bf16[2,256,2048]{1,2,0:T(8,128)(2,1)} %copy-done.8) | copy-start | bytes 6291460
  108.1 32.7 %copy-start.49 = (pred[256,256]{0,1:T(8,128)(4,1)}, pred[256,256]{0,1:T(8,128)(4,1)S(1)}, u32[]{:S(2)}) copy-start(pred[256,256]{0,1:T(8,128)(4,1)S(1)} %get-tuple-element.327) | copy-start | bytes 196612
  108.1 58.3 %copy-start.46 = (pred[256,256]{0,1:T(8,128)(4,1)}, pred[256,256]{0,1:T(8,128)(4,1)S(1)}, u32[]{:S(2)}) copy-start(pred[256,256]{0,1:T(8,128)(4,1)S(1)} %get-tuple-element.329) | copy-start | bytes 196612
  108.1 62.0 %copy-start.43 = (pred[256,256]{0,1:T(8,128)(4,1)}, pred[256,256]{0,1:T(8,128)(4,1)S(1)}, u32[]{:S(2)}) copy-start(pred[256,256]{0,1:T(8,128)(4,1)S(1)} %get-tuple-element.331) | copy-start | bytes 196612
  108.1 98.4 %copy-start.40 = (pred[256,256]{0,1:T(8,128)(4,1)}, pred[256,256]{0,1:T(8,128)(4,1)S(1)}, u32[]{:S(2)}) copy-start(pred[256,256]{0,1:T(8,128)(4,1)S(1)} %get-tuple-element.333) | copy-start | bytes 196612
  108.1 100.5 %copy-start.37 = (pred[256,256]{0,1:T(8,128)(4,1)}, pred[256,256]{0,1:T(8,128)(4,1)S(1)}, u32[]{:S(2)}) copy-start(pred[256,256]{0,1:T(8,128)(4,1)S(1)} %get-tuple-element.335) | copy-start | bytes 196612
  132.8 29.7 %collective-permute-start.5 = (bf16[2,256,2048]{1,2,0:T(8,128)(2,1)}, bf16[2,256,2048]{1,2,0:T(8,128)(2,1)S(1)}, u32[]{:S(2)}, u32[]{:S(2)}) collective-permute-start(bf16[2,256,2048]{1,2,0:T(8,128)(2,1)} %collective-permute-done.4), channel_id=1, source_target_pairs={{0,1},{1,2},{2,3},{3,4},{4,5},{5,6},{6,7},{7,8},{8,9},{9,10},{10,1... | collective-permute-start | bytes 6291464 | tf_op jit(solution)/shard_map/ppermute | solution.py:38
  136.2 106.6 %copy-start.58 = (f32[16,256]{1,0:T(8,128)}, f32[16,256]{1,0:T(8,128)S(1)}, u32[]{:S(2)}) copy-start(f32[16,256]{1,0:T(8,128)S(1)} %get-tuple-element.357) | copy-start | bytes 49156
  136.3 107.7 %copy-start.6 = (f32[16,256,256]{1,2,0:T(8,128)}, f32[16,256,256]{1,2,0:T(8,128)S(1)}, u32[]{:S(2)}) copy-start(f32[16,256,256]{1,2,0:T(8,128)S(1)} %get-tuple-element.358) | copy-start | bytes 12582916
  162.5 42.6 %collective-permute-start.6 = (bf16[2,256,2048]{1,2,0:T(8,128)(2,1)S(1)}, bf16[2,256,2048]{1,2,0:T(8,128)(2,1)S(1)}, u32[]{:S(2)}, u32[]{:S(2)}) collective-permute-start(bf16[2,256,2048]{1,2,0:T(8,128)(2,1)S(1)} %collective-permute-done.5), channel_id=1, source_target_pairs={{0,1},{1,2},{2,3},{3,4},{4,5},{5,6},{6,7},{7,8},{8,9},{9,10},{10,1... | collective-permute-start | bytes 6291464 | tf_op jit(solution)/shard_map/ppermute | solution.py:38
  205.1 35.6 %collective-permute-start.7 = (bf16[2,256,2048]{1,2,0:T(8,128)(2,1)S(1)}, bf16[2,256,2048]{1,2,0:T(8,128)(2,1)S(1)}, u32[]{:S(2)}, u32[]{:S(2)}) collective-permute-start(bf16[2,256,2048]{1,2,0:T(8,128)(2,1)S(1)} %collective-permute-done.6), channel_id=1, source_target_pairs={{0,1},{1,2},{2,3},{3,4},{4,5},{5,6},{6,7},{7,8},{8,9},{9,10},{10,1... | collective-permute-start | bytes 6291464 | tf_op jit(solution)/shard_map/ppermute | solution.py:38
  287.6 73.6 %copy-start.12 = (bf16[256,2048]{1,0:T(8,128)(2,1)S(1)}, bf16[256,2048]{1,0:T(8,128)(2,1)}, u32[]{:S(2)}) copy-start(bf16[256,2048]{1,0:T(8,128)(2,1)} %param.17) | copy-start | bytes 3145732
  405.0 37.7 %copy-start.3 = (f32[16,128]{1,0:T(8,128)S(1)}, f32[16,128]{1,0:T(8,128)}, u32[]{:S(2)}) copy-start(f32[16,128]{1,0:T(8,128)} %param.21) | copy-start | bytes 24580
  (85 other events, 280.3 us)
Sparse Core Ops, SparseCore 0:
  88.8 113.5 all-gather.5
  284.5 119.3 all-gather.7
where the time goes:
time: 687 us; the launch traced here: 676 us
  matrix products  227 us (33%)
  waiting for transfers between devices  190 us (28%)
  other arithmetic  104 us (15%)
  blocking collectives  68.2 us (10%)
  local copies, waits for them, and re-layouts  54.8 us (8%)
  between operations  16.6 us (2%)
  starting transfers between devices  10.5 us (2%)
    ppermute x8, waiting for transfers between devices, passed_along(): lax.ppermute(value, axis, [(source, source + steps) for source in range(f...  177 us
    dot_general x32, matrix products, span_update(): jnp.einsum('hcd,hed->hce', search, gram_start, precision=exact_mode)  73.5 us
    unnamed x1, blocking collectives  68.2 us
    add x30, other arithmetic, combine_pair(): jnp.exp(later[0])[:, None, None] * earlier[1] + later[1]  57.1 us
    dot_general x32, matrix products, span_update(): jnp.einsum('hjd,hid->hji', search, k_heads, precision=exact_mode)  32.5 us
    dot_general x9, matrix products, fold_block(): jnp.einsum('hqk,khd->hqd', weights.astype(jnp.bfloat16), value_rows, pref...  24 us
    dot_general x32, matrix products, span_update(): jnp.einsum('hji,hid->hjd', decay_mix * operator_products, k_heads, precis...  20.8 us
    dot_general x4, matrix products, span_update(): jnp.einsum('hid,hie->hde', v_heads * tail_weight, k_heads, precision=exac...  17.6 us
  transfers between devices with their start and end apart: 10, of which 9 were waited for; matrix products, arithmetic and copies ran while one was open for 17% of the time, Pallas kernels for 0%

commit v1 on v0

--- a/solution.py
+++ b/solution.py
@@ -1,6 +1,11 @@
+import functools
+import math
+
 import jax
 import jax.numpy as jnp
 from jax import lax
+from jax.experimental import pallas as pl
+from jax.experimental.pallas import tpu as pltpu
 from jax.sharding import PartitionSpec as P
 
 WINDOW = 2048
@@ -139,6 +144,243 @@
     return (earlier[0] + later[0], jnp.exp(later[0])[:, None, None] * earlier[1] + later[1])
 
 
+def split_cat(value, axis):
+    high = value.astype(jnp.bfloat16)
+    low = (value - high.astype(jnp.float32)).astype(jnp.bfloat16)
+    return jnp.concatenate([high, low], axis=axis)
+
+
+def dot_nn(a, b):
+    return lax.dot_general(a, b, (((1,), (0,)), ((), ())), preferred_element_type=jnp.float32)
+
+
+def dot_nt(a, b):
+    return lax.dot_general(a, b, (((1,), (1,)), ((), ())), preferred_element_type=jnp.float32)
+
+
+def attend_kernel(qkv_ref, out_ref, *, rows, reach):
+    i = pl.program_id(0)
+    size = qkv_ref.shape[-1]
+    factor = size ** (-0.5) * math.log2(math.e)
+    col = lax.broadcasted_iota(jnp.int32, (rows, rows), 1)
+    row = lax.broadcasted_iota(jnp.int32, (rows, rows), 0)
+
+    def run(first, count, full):
+        q = qkv_ref[i, pl.ds(0, rows), :]
+        scores = []
+        for c in range(count):
+            s = dot_nt(q, qkv_ref[first + c, pl.ds(rows, rows), :])
+            if full:
+                if c == 0:
+                    s = jnp.where(col > row, s, masked_score)
+                elif c == count - 1:
+                    s = jnp.where(col <= row, s, masked_score)
+            else:
+                s = jnp.where(col - row <= (i - c) * rows, s, masked_score)
+            scores.append(s)
+        top = jnp.max(functools.reduce(jnp.maximum, scores), axis=-1, keepdims=True)
+        total = None
+        acc = None
+        for c in range(count):
+            w = jnp.exp2((scores[c] - top) * factor)
+            part = dot_nn(w.astype(jnp.bfloat16), qkv_ref[first + c, pl.ds(2 * rows, rows), :])
+            total = w if total is None else total + w
+            acc = part if acc is None else acc + part
+        total = jnp.sum(total, axis=-1, keepdims=True)
+        out_ref[0] = (acc / total).astype(out_ref.dtype)
+
+    bounds = sorted({max(1, reach // 2), reach})
+    low = 0
+    for bound in bounds:
+        pl.when((i >= low) & (i < bound))(functools.partial(run, 0, bound, False))
+        low = bound
+    pl.when(i >= reach)(lambda: run(i - reach, reach + 1, True))
+
+
+def attend(qkv, rows, reach):
+    slabs, _, size = qkv.shape
+    return pl.pallas_call(
+        functools.partial(attend_kernel, rows=rows, reach=reach),
+        grid=(slabs,),
+        in_specs=[pl.BlockSpec(qkv.shape, lambda i: (0, 0, 0))],
+        out_specs=pl.BlockSpec((1, rows, size), lambda i: (i, 0, 0)),
+        out_shape=jax.ShapeDtypeStruct((slabs, rows, size), jnp.bfloat16),
+        name="attend",
+    )(qkv)
+
+
+def states_kernel(k_ref, x_ref, w_ref, out_ref):
+    slabs, rows, size = k_ref.shape
+    state = jnp.zeros((size, size), jnp.float32)
+    for j in range(slabs):
+        out_ref[j] = state.astype(out_ref.dtype)
+        if j == slabs - 1:
+            break
+        weighted = jnp.transpose(k_ref[j].astype(jnp.float32)) * w_ref[j, 0:1, :]
+        x = x_ref[j]
+        fresh = dot_nn(split_cat(weighted, 1), jnp.concatenate([x, x], axis=0))
+        state = w_ref[j, 1:2, :size] * state + fresh
+
+
+def states(keys, others, weights):
+    slabs, rows, size = keys.shape
+    return pl.pallas_call(
+        states_kernel,
+        out_shape=jax.ShapeDtypeStruct((slabs, size, size), jnp.bfloat16),
+        name="states",
+    )(keys, others, weights)
+
+
+def solve_kernel(q_ref, k_ref, rate_ref, gate_ref, ridge_ref, gram_ref, x_ref, p_ref):
+    rows = q_ref.shape[0]
+    heads, size = ridge_ref.shape[1:]
+    causal = lax.broadcasted_iota(jnp.int32, (rows, rows), 0) >= lax.broadcasted_iota(
+        jnp.int32, (rows, rows), 1
+    )
+    held = []
+    for h in range(heads):
+        cols = slice(h * size, (h + 1) * size)
+        key = k_ref[:, cols]
+        by_col = jnp.broadcast_to(rate_ref[0, h : h + 1, :], (rows, rows))
+        by_row = jnp.transpose(by_col)
+        mix = (
+            jnp.where(causal, jnp.exp(jnp.where(causal, by_row - by_col, 0.0)), 0.0)
+            * gate_ref[0, h : h + 1, :]
+        )
+        gram = gram_ref[h]
+        query = q_ref[:, cols].astype(jnp.float32)
+        held.append(
+            dict(
+                wide=jnp.concatenate([key, key], axis=1),
+                tall=jnp.concatenate([key, key], axis=0),
+                gram=jnp.concatenate([gram, gram], axis=0),
+                mix=mix,
+                scale=jnp.exp(by_row[:, :size]),
+                ridge=ridge_ref[0, h : h + 1, :],
+                x=jnp.zeros_like(query),
+                r=query,
+                p=query,
+                rr=jnp.sum(query * query, axis=-1, keepdims=True),
+            )
+        )
+    for _ in range(CG_ITERS):
+        for s in held:
+            p = s["p"]
+            parts = split_cat(p, 1)
+            products = split_cat(s["mix"] * dot_nt(parts, s["wide"]), 1)
+            image = (
+                s["scale"] * dot_nn(parts, s["gram"]) + dot_nn(products, s["tall"]) + s["ridge"] * p
+            )
+            alpha = s["rr"] / (jnp.sum(p * image, axis=-1, keepdims=True) + 1e-6)
+            s["x"] = s["x"] + alpha * p
+            s["r"] = s["r"] - alpha * image
+            new = jnp.sum(s["r"] * s["r"], axis=-1, keepdims=True)
+            s["p"] = s["r"] + (new / (s["rr"] + 1e-6)) * p
+            s["rr"] = new
+    for h, s in enumerate(held):
+        x_ref[h] = (s["scale"] * s["x"]).astype(x_ref.dtype)
+        p_ref[h] = (s["mix"] * dot_nt(split_cat(s["x"], 1), s["wide"])).astype(p_ref.dtype)
+
+
+def solve(queries, keys, rates, gates, ridge, gram, group):
+    rows = queries.shape[0]
+    heads, size = ridge.shape
+    steps = heads // group
+
+    def packed(a):
+        return a.reshape(steps, group, a.shape[-1])
+
+    def small(width):
+        return pl.BlockSpec((1, group, width), lambda i: (i, 0, 0))
+
+    wide = pl.BlockSpec((rows, group * size), lambda i: (0, i))
+    return pl.pallas_call(
+        solve_kernel,
+        grid=(steps,),
+        in_specs=[
+            wide,
+            wide,
+            small(rows),
+            small(rows),
+            small(size),
+            pl.BlockSpec((group, size, size), lambda i: (i, 0, 0)),
+        ],
+        out_specs=[
+            pl.BlockSpec((group, rows, size), lambda i: (i, 0, 0)),
+            pl.BlockSpec((group, rows, rows), lambda i: (i, 0, 0)),
+        ],
+        out_shape=[
+            jax.ShapeDtypeStruct((heads, rows, size), jnp.bfloat16),
+            jax.ShapeDtypeStruct((heads, rows, rows), jnp.bfloat16),
+        ],
+        name="solve",
+    )(queries, keys, packed(rates), packed(gates), packed(ridge), gram)
+
+
+def finish_kernel(x_ref, p_ref, v_ref, cross_ref, att_ref, out_ref):
+    heads, rows, size = x_ref.shape
+    for h in range(heads):
+        cols = slice(h * size, (h + 1) * size)
+        value = v_ref[h]
+        att_ref[:, cols] = value
+        out_ref[:, cols] = (dot_nn(x_ref[h], cross_ref[h]) + dot_nn(p_ref[h], value)).astype(
+            out_ref.dtype
+        )
+
+
+def finish(x, products, values, cross, group):
+    heads, rows, size = x.shape
+
+    def spec(a):
+        return pl.BlockSpec((group,) + a.shape[1:], lambda i: (i, 0, 0))
+
+    flat = pl.BlockSpec((rows, group * size), lambda i: (0, i))
+    shape = jax.ShapeDtypeStruct((rows, heads * size), jnp.bfloat16)
+    return pl.pallas_call(
+        finish_kernel,
+        grid=(heads // group,),
+        in_specs=[spec(x), spec(products), spec(values), spec(cross)],
+        out_specs=[flat, flat],
+        out_shape=[shape, shape],
+        name="finish",
+    )(x, products, values, cross)
+
+
+def exchange(value):
+    return lax.all_to_all(value, "seq", 0, 0, tiled=True)
+
+
+def by_head(value, heads):
+    rows = value.shape[0]
+    return jnp.transpose(value.reshape(rows, heads, -1), (1, 0, 2))
+
+
+def head_body(
+    attn_query, attn_key, attn_value, mesa_query, mesa_key, log_decay, input_gate, regularizer
+):
+    rows = attn_query.shape[0]
+    heads, size = regularizer.shape
+    lower = jnp.tril(jnp.ones((rows, rows), jnp.float32))
+    rates = jnp.einsum("th,st->hs", log_decay, lower, precision=exact_mode)
+    gates = jnp.transpose(input_gate)
+    last = rates[:, -1:]
+    weights = jnp.stack(
+        [jnp.exp(last - rates) * gates, jnp.broadcast_to(jnp.exp(last), rates.shape)], axis=1
+    )
+    qkv = exchange(
+        jnp.concatenate([by_head(a, heads) for a in (attn_query, attn_key, attn_value)], axis=1)
+    )
+    weights = exchange(weights)
+    keys = exchange(by_head(mesa_key, heads))
+    gram = exchange(states(keys, keys, weights))
+    values = attend(qkv, rows, WINDOW // rows)
+    local_values = exchange(values)
+    cross = exchange(states(keys, values, weights))
+    group = 2 if heads % 2 == 0 else 1
+    x, products = solve(mesa_query, mesa_key, rates, gates, regularizer, gram, group)
+    return tuple(finish(x, products, local_values, cross, group))
+
+
 def body(
     attn_query, attn_key, attn_value, mesa_query, mesa_key, log_decay, input_gate, regularizer
 ):
@@ -192,8 +434,16 @@
 
 
 def solution(mesh):
+    def chosen(*arrays):
+        rows = arrays[0].shape[0]
+        heads, size = arrays[-1].shape
+        fits = WINDOW % rows == 0 and rows % 128 == 0 and size == 128
+        if heads == mesh.shape["seq"] and fits:
+            return head_body(*arrays)
+        return body(*arrays)
+
     return jax.shard_map(
-        body,
+        chosen,
         mesh=mesh,
         in_specs=(
             P(("groups", "seq"), None),

time: 687 us -> 221 us (0.32); the launches traced: 676 us -> 219 us
  matrix products: 227 us -> 0.27 us
  waiting for transfers between devices: 190 us -> 79.9 us
  other arithmetic: 104 us -> 4.39 us
  Pallas kernels: 0 us -> 69.8 us
  blocking collectives: 68.2 us -> 18.8 us
  local copies, waits for them, and re-layouts: 54.8 us -> 13.9 us
  starting transfers between devices: 10.5 us -> 30.9 us
  between operations: 16.6 us -> 0.74 us
    dot_general x136 -> x1, matrix products: 227 us -> 0.27 us  [head_body(): rates = jnp.einsum('th,st->hs', log_decay, lower, precision=exact_mode)]
    ppermute x8 -> x0, waiting for transfers between devices: 177 us -> none  [passed_along(): lax.ppermute(value, axis, [(source, source + steps) for source in range(f...]
    all_to_all x0 -> x5, waiting for transfers between devices: none -> 79.9 us  [exchange(): return lax.all_to_all(value, 'seq', 0, 0, tiled=True)]
    add x72 -> x0, other arithmetic: 70.8 us -> none  [the longest x30 57.1 us: combine_pair(): jnp.exp(later[0])[:, None, None] * earlier[1] + later[1]]
    pallas_call x0 -> x5, Pallas kernels: none -> 69.8 us  [the longest x1 36.3 us: solve(): pl.pallas_call(solve_kernel, grid=(steps,), in_specs=[wide, wide, small(r...]
    unnamed x1 -> x0, blocking collectives: 68.2 us -> none
    all_to_all x0 -> x5, starting transfers between devices: none -> 30.9 us  [exchange(): return lax.all_to_all(value, 'seq', 0, 0, tiled=True)]
    reduce_sum x34 -> x0, other arithmetic: 21.6 us -> none  [the longest x28 11.6 us: span_update(): norm_next = jnp.sum(remain * remain, axis=-1, keepdims=True)]
  transfers between devices with their start and end apart: 10 -> 5, of which waited for: 9 -> 2; matrix products, arithmetic and copies ran while one was open for 17% -> 6% of each run, Pallas kernels for 0% -> 29%
where the time goes in v1:
time: 221 us; the launch traced here: 219 us
  waiting for transfers between devices  79.9 us (36%)
  Pallas kernels  69.8 us (32%)
  starting transfers between devices  30.9 us (14%)
  blocking collectives  18.8 us (9%)
  local copies, waits for them, and re-layouts  13.9 us (6%)
  other arithmetic  4.39 us (2%)
    all_to_all x5, waiting for transfers between devices, exchange(): return lax.all_to_all(value, 'seq', 0, 0, tiled=True)  79.9 us
    pallas_call x1, Pallas kernels, solve(): pl.pallas_call(solve_kernel, grid=(steps,), in_specs=[wide, wide, small(r...  36.3 us
    all_to_all x5, starting transfers between devices, exchange(): return lax.all_to_all(value, 'seq', 0, 0, tiled=True)  30.9 us
    pallas_call x1, Pallas kernels, attend(): pl.pallas_call(functools.partial(attend_kernel, rows=rows, reach=reach),...  20.4 us
    all_to_all x1, blocking collectives, exchange(): return lax.all_to_all(value, 'seq', 0, 0, tiled=True)  18.8 us
    unnamed x18, local copies, waits for them, and re-layouts  7.74 us
    pallas_call x1, Pallas kernels, finish(): pl.pallas_call(finish_kernel, grid=(heads // group,), in_specs=[spec(x),...  6.77 us
    pallas_call x2, Pallas kernels, states(): pl.pallas_call(states_kernel, out_shape=jax.ShapeDtypeStruct((slabs, size...  6.39 us
  transfers between devices with their start and end apart: 5, of which 2 were waited for; matrix products, arithmetic and copies ran while one was open for 6% of the time, Pallas kernels for 29%

profile of v1, /device:TPU:29, one launch (start us, length us, event | category | flops | bytes accessed | tf_op | source)
XLA Modules:
  0.0 218.8 jit_solution(16747232552445135015)
XLA Ops:
  0.6 0.7 copy-done
  1.9 0.8 exponential_multiply_fusion
  3.4 6.3 %all-to-all-start.1 = ((f32[16,2,256]{2,1,0:T(2,128)}), f32[16,2,256]{2,1,0:T(2,128)S(1)}, u32[]{:S(2)}, u32[]{:S(2)}) async-start(f32[16,2,256]{2,1,0:T(2,128)} %pad_maximum_fusion.1), calls=%async_computation.1 | async-start | bytes 65536 | tf_op jit(solution)/shard_map/all_to_all | solution.py:350
  9.7 1.6 copy.10
  11.3 1.3 copy.11
  12.6 7.4 %all-to-all-start = ((bf16[16,256,128]{2,1,0:T(8,128)(2,1)}), bf16[16,256,128]{2,1,0:T(8,128)(2,1)S(1)}, u32[]{:S(2)}, u32[]{:S(2)}) async-start(bf16[16,256,128]{2,1,0:T(8,128)(2,1)} %bitcast.4), calls=%async_computation | async-start | bytes 2097152 | tf_op jit(solution)/shard_map/all_to_all | solution.py:350
  21.2 1.5 copy.14
  22.7 1.3 copy.15
  24.0 1.5 copy.16
  25.5 1.3 copy.17
  26.8 2.9 %pad_maximum_fusion = bf16[16,768,128]{2,1,0:T(8,128)(2,1)} fusion(bf16[16,256,128]{2,1,0:T(8,128)(2,1)} %bitcast.20, bf16[16,256,128]{2,1,0:T(8,128)(2,1)} %bitcast.19, bf16[16,256,128]{2,1,0:T(8,128)(2,1)S(1)} %bitcast.18), kind=kLoop, calls=%fused_computation | loop fusion | flops 9437184 | bytes 6291456 | tf_op jit(solution)/shard_map/concatenate | solution.py:371
  29.7 14.1 %all-to-all-done.k_ref.x_ref = bf16[16,256,128]{2,1,0:T(8,128)(2,1)S(1)} async-done(((bf16[16,256,128]{2,1,0:T(8,128)(2,1)}), bf16[16,256,128]{2,1,0:T(8,128)(2,1)S(1)}, u32[]{:S(2)}, u32[]{:S(2)}) %all-to-all-start) | async-done | bytes 1048608 | tf_op jit(solution)/shard_map/all_to_all | solution.py:350
  43.9 1.0 copy-done.1
  44.9 5.7 %all-to-all-start.3 = ((bf16[16,768,128]{2,1,0:T(8,128)(2,1)}), bf16[16,768,128]{2,1,0:T(8,128)(2,1)}, u32[]{:S(2)}, u32[]{:S(2)}) async-start(bf16[16,768,128]{2,1,0:T(8,128)(2,1)} %pad_maximum_fusion), calls=%async_computation.3 | async-start | bytes 6291456 | tf_op jit(solution)/shard_map/all_to_all | solution.py:350
  50.6 3.2 %states.2 = bf16[16,128,128]{2,1,0:T(8,128)(2,1)} custom-call(bf16[16,256,128]{2,1,0:T(8,128)(2,1)} %copy-done.1, bf16[16,256,128]{2,1,0:T(8,128)(2,1)} %copy-done.1, f32[16,2,256]{2,1,0:T(2,128)} %copy-done.5), custom_call_target="tpu_custom_call" | custom-call | tf_op jit(solution)/shard_map/states/pallas_call | solution.py:227
  53.8 65.8 %all-to-all-done.3.qkv_ref = bf16[16,768,128]{2,1,0:T(8,128)(2,1)} async-done(((bf16[16,768,128]{2,1,0:T(8,128)(2,1)}), bf16[16,768,128]{2,1,0:T(8,128)(2,1)}, u32[]{:S(2)}, u32[]{:S(2)}) %all-to-all-start.3) | async-done | bytes 3145760 | tf_op jit(solution)/shard_map/all_to_all | solution.py:350
  119.6 5.7 %all-to-all-start.2 = ((bf16[16,128,128]{2,1,0:T(8,128)(2,1)}), bf16[16,128,128]{2,1,0:T(8,128)(2,1)S(1)}, u32[]{:S(2)}, u32[]{:S(2)}) async-start(bf16[16,128,128]{2,1,0:T(8,128)(2,1)} %states.2), calls=%async_computation.2 | async-start | bytes 1048576 | tf_op jit(solution)/shard_map/all_to_all | solution.py:350
  125.4 20.4 %attend.1.x_ref = bf16[16,256,128]{2,1,0:T(8,128)(2,1)} custom-call(bf16[16,768,128]{2,1,0:T(8,128)(2,1)} %all-to-all-done.3.qkv_ref), custom_call_target="tpu_custom_call" | custom-call | tf_op jit(solution)/shard_map/attend/pallas_call | solution.py:202
  145.8 3.2 %states.3 = bf16[16,128,128]{2,1,0:T(8,128)(2,1)} custom-call(bf16[16,256,128]{2,1,0:T(8,128)(2,1)} %copy-done.1, bf16[16,256,128]{2,1,0:T(8,128)(2,1)} %attend.1.x_ref, f32[16,2,256]{2,1,0:T(2,128)} %copy-done.5), custom_call_target="tpu_custom_call" | custom-call | tf_op jit(solution)/shard_map/states/pallas_call | solution.py:227
  148.9 18.8 %all_to_all.30.cross_ref = bf16[16,128,128]{2,1,0:T(8,128)(2,1)} all-to-all(bf16[16,128,128]{2,1,0:T(8,128)(2,1)} %states.3), channel_id=1, replica_groups=mesh['groups'=2,'seq'=16] {'seq'}, dimensions={0} | all-to-all | bytes 1048576 | tf_op jit(solution)/shard_map/all_to_all | solution.py:350
  167.7 5.7 %all-to-all-start.4 = ((bf16[16,256,128]{2,1,0:T(8,128)(2,1)}), bf16[16,256,128]{2,1,0:T(8,128)(2,1)S(1)}, u32[]{:S(2)}, u32[]{:S(2)}) async-start(bf16[16,256,128]{2,1,0:T(8,128)(2,1)} %attend.1.x_ref), calls=%async_computation.4 | async-start | bytes 2097152 | tf_op jit(solution)/shard_map/all_to_all | solution.py:350
  174.7 36.3 %solve.1 = (bf16[16,256,128]{2,1,0:T(8,128)(2,1)}, bf16[16,256,256]{2,1,0:T(8,128)(2,1)}) custom-call(bf16[256,2048]{1,0:T(8,128)(2,1)} %q_ref.1, bf16[256,2048]{1,0:T(8,128)(2,1)} %k_ref.1, f32[8,2,256]{2,1,0:T(2,128)} %reshape.28.rate_ref, f32[8,2,256]{2,1,0:T(2,128)} %reshape.29.gate_ref, f32[8,2,128]{2,1,0:T(2,128)} %bitcast.22, ...), custom_call_target="tpu_custom_call" | custom-call | tf_op jit(solution)/shard_map/solve/pallas_call | solution.py:297
  211.0 1.0 copy-done.2
  212.0 6.8 %finish.1 = (bf16[256,2048]{1,0:T(8,128)(2,1)}, bf16[256,2048]{1,0:T(8,128)(2,1)}) custom-call(bf16[16,256,128]{2,1,0:T(8,128)(2,1)} %get-tuple-element.4.x_ref, bf16[16,256,256]{2,1,0:T(8,128)(2,1)} %get-tuple-element.5.p_ref, bf16[16,256,128]{2,1,0:T(8,128)(2,1)} %copy-done.2, bf16[16,128,128]{2,1,0:T(8,128)(2,1)} %all_to_all.30.cross_ref), custom_call_target="tpu_custom_call" | custom-call | tf_op jit(solution)/shard_map/finish/pallas_call | solution.py:339
  (23 shorter events, 3.7 us)
Async XLA Ops:
  0.6 0.7 copy-start
  3.4 9.2 %all-to-all-start.1 = ((f32[16,2,256]{2,1,0:T(2,128)}), f32[16,2,256]{2,1,0:T(2,128)S(1)}, u32[]{:S(2)}, u32[]{:S(2)}) async-start(f32[16,2,256]{2,1,0:T(2,128)} %pad_maximum_fusion.1), calls=%async_computation.1 | async-start | bytes 65536 | tf_op jit(solution)/shard_map/all_to_all | solution.py:350
  9.7 10.3 %copy-start.4 = (bf16[256,2048]{1,0:T(8,128)(2,1)S(1)}, bf16[256,2048]{1,0:T(8,128)(2,1)}, u32[]{:S(2)}) copy-start(bf16[256,2048]{1,0:T(8,128)(2,1)} %param.8) | copy-start | bytes 3145732
  12.6 8.6 %copy-start.5 = (f32[16,2,256]{2,1,0:T(2,128)}, f32[16,2,256]{2,1,0:T(2,128)S(1)}, u32[]{:S(2)}) copy-start(f32[16,2,256]{2,1,0:T(2,128)S(1)} %all-to-all-done.1.w_ref) | copy-start | bytes 98308
  12.6 31.3 %all-to-all-start = ((bf16[16,256,128]{2,1,0:T(8,128)(2,1)}), bf16[16,256,128]{2,1,0:T(8,128)(2,1)S(1)}, u32[]{:S(2)}, u32[]{:S(2)}) async-start(bf16[16,256,128]{2,1,0:T(8,128)(2,1)} %bitcast.4), calls=%async_computation | async-start | bytes 2097152 | tf_op jit(solution)/shard_map/all_to_all | solution.py:350
  43.9 1.0 copy-start.1
  44.9 74.8 %all-to-all-start.3 = ((bf16[16,768,128]{2,1,0:T(8,128)(2,1)}), bf16[16,768,128]{2,1,0:T(8,128)(2,1)}, u32[]{:S(2)}, u32[]{:S(2)}) async-start(bf16[16,768,128]{2,1,0:T(8,128)(2,1)} %pad_maximum_fusion), calls=%async_computation.3 | async-start | bytes 6291456 | tf_op jit(solution)/shard_map/all_to_all | solution.py:350
  119.6 29.3 %all-to-all-start.2 = ((bf16[16,128,128]{2,1,0:T(8,128)(2,1)}), bf16[16,128,128]{2,1,0:T(8,128)(2,1)S(1)}, u32[]{:S(2)}, u32[]{:S(2)}) async-start(bf16[16,128,128]{2,1,0:T(8,128)(2,1)} %states.2), calls=%async_computation.2 | async-start | bytes 1048576 | tf_op jit(solution)/shard_map/all_to_all | solution.py:350
  145.8 28.3 %copy-start.6 = (f32[256,16]{0,1:T(8,128)S(1)}, f32[256,16]{0,1:T(8,128)}, u32[]{:S(2)}) copy-start(f32[256,16]{0,1:T(8,128)} %param.14) | copy-start | bytes 49156
  148.9 25.8 %copy-start.3 = (bf16[16,128,128]{2,1,0:T(8,128)(2,1)}, bf16[16,128,128]{2,1,0:T(8,128)(2,1)S(1)}, u32[]{:S(2)}) copy-start(bf16[16,128,128]{2,1,0:T(8,128)(2,1)S(1)} %all-to-all-done.2.gram_ref) | copy-start | bytes 1572868
  167.7 43.3 %all-to-all-start.4 = ((bf16[16,256,128]{2,1,0:T(8,128)(2,1)}), bf16[16,256,128]{2,1,0:T(8,128)(2,1)S(1)}, u32[]{:S(2)}, u32[]{:S(2)}) async-start(bf16[16,256,128]{2,1,0:T(8,128)(2,1)} %attend.1.x_ref), calls=%async_computation.4 | async-start | bytes 2097152 | tf_op jit(solution)/shard_map/all_to_all | solution.py:350
  211.0 1.0 copy-start.2

commit v2 on v1

--- a/solution.py
+++ b/solution.py
@@ -158,7 +158,70 @@
     return lax.dot_general(a, b, (((1,), (1,)), ((), ())), preferred_element_type=jnp.float32)
 
 
-def attend_kernel(qkv_ref, out_ref, *, rows, reach):
+def fresh_state(packed, others):
+    rows = others.shape[0]
+    keys = packed[:rows].astype(jnp.float32)
+    extra = packed[rows:].astype(jnp.float32)
+    count = rows // packed.shape[1]
+    weights = extra[:count] + extra[count : 2 * count]
+    weights = jnp.concatenate([weights[c : c + 1] for c in range(count)], axis=1)
+    decay = extra[2 * count : 2 * count + 1] + extra[2 * count + 1 : 2 * count + 2]
+    weighted = split_cat(jnp.transpose(keys) * weights, 1)
+    return decay, dot_nn(weighted, jnp.concatenate([others, others], axis=0))
+
+
+def pack_keys_kernel(k_ref, rate_ref, gate_ref, out_ref, total_ref, gate_out_ref):
+    heads, height, size = out_ref.shape
+    rows = k_ref.shape[0]
+    count = rows // size
+    at = lax.broadcasted_iota(jnp.int32, (rows, rows), 0)
+    lower = (at >= lax.broadcasted_iota(jnp.int32, (rows, rows), 1)).astype(jnp.float32)
+    totals = jnp.transpose(
+        lax.dot_general(
+            lower,
+            rate_ref[...],
+            (((1,), (0,)), ((), ())),
+            precision=exact_mode,
+            preferred_element_type=jnp.float32,
+        )
+    )
+    gates = jnp.transpose(gate_ref[...])
+    total_ref[...] = totals
+    gate_out_ref[...] = gates
+    last = totals[:, rows - 1 :]
+    weights = jnp.exp(last - totals) * gates
+    decays = jnp.broadcast_to(jnp.exp(last), (heads, size))
+    place = lax.broadcasted_iota(jnp.int32, (height - rows, size), 0)
+    for h in range(heads):
+        pieces = [weights[h : h + 1, c * size : (c + 1) * size] for c in range(count)]
+        high = [p.astype(jnp.bfloat16).astype(jnp.float32) for p in pieces]
+        decay = decays[h : h + 1]
+        decay_high = decay.astype(jnp.bfloat16).astype(jnp.float32)
+        lines = high + [p - q for p, q in zip(pieces, high)] + [decay_high, decay - decay_high]
+        tile = jnp.zeros((height - rows, size), jnp.float32)
+        for n, line in enumerate(lines):
+            tile = jnp.where(place == n, line, tile)
+        out_ref[h, :rows, :] = k_ref[:, h * size : (h + 1) * size]
+        out_ref[h, rows:, :] = tile.astype(jnp.bfloat16)
+
+
+def pack_keys(keys, rates, gates, size):
+    rows, features = keys.shape
+    heads = features // size
+    spare = -(-(2 * (rows // size) + 2) // 16) * 16
+    small = jax.ShapeDtypeStruct((heads, rows), jnp.float32)
+    return pl.pallas_call(
+        pack_keys_kernel,
+        out_shape=[
+            jax.ShapeDtypeStruct((heads, rows + spare, size), jnp.bfloat16),
+            small,
+            small,
+        ],
+        name="pack_keys",
+    )(keys, rates, gates)
+
+
+def attend_kernel(qkv_ref, key_ref, out_ref, state_ref, *, rows, reach):
     i = pl.program_id(0)
     size = qkv_ref.shape[-1]
     factor = size ** (-0.5) * math.log2(math.e)
@@ -187,9 +250,18 @@
             total = w if total is None else total + w
             acc = part if acc is None else acc + part
         total = jnp.sum(total, axis=-1, keepdims=True)
-        out_ref[0] = (acc / total).astype(out_ref.dtype)
-
-    bounds = sorted({max(1, reach // 2), reach})
+        value = (acc / total).astype(out_ref.dtype)
+        out_ref[0, :rows, :] = value
+        decay, fresh = fresh_state(key_ref[i], value)
+        state = state_ref[...]
+        out_ref[0, rows:, :] = state.astype(out_ref.dtype)
+        state_ref[...] = decay * state + fresh
+
+    @pl.when(i == 0)
+    def _():
+        state_ref[...] = jnp.zeros_like(state_ref)
+
+    bounds = sorted({max(1, reach * n // 4) for n in range(1, 5)})
     low = 0
     for bound in bounds:
         pl.when((i >= low) & (i < bound))(functools.partial(run, 0, bound, False))
@@ -197,38 +269,39 @@
     pl.when(i >= reach)(lambda: run(i - reach, reach + 1, True))
 
 
-def attend(qkv, rows, reach):
+def attend(qkv, keys, rows, reach):
     slabs, _, size = qkv.shape
     return pl.pallas_call(
         functools.partial(attend_kernel, rows=rows, reach=reach),
         grid=(slabs,),
-        in_specs=[pl.BlockSpec(qkv.shape, lambda i: (0, 0, 0))],
-        out_specs=pl.BlockSpec((1, rows, size), lambda i: (i, 0, 0)),
-        out_shape=jax.ShapeDtypeStruct((slabs, rows, size), jnp.bfloat16),
+        in_specs=[
+            pl.BlockSpec(qkv.shape, lambda i: (0, 0, 0)),
+            pl.BlockSpec(keys.shape, lambda i: (0, 0, 0)),
+        ],
+        out_specs=pl.BlockSpec((1, rows + size, size), lambda i: (i, 0, 0)),
+        out_shape=jax.ShapeDtypeStruct((slabs, rows + size, size), jnp.bfloat16),
+        scratch_shapes=[pltpu.VMEM((size, size), jnp.float32)],
         name="attend",
-    )(qkv)
-
-
-def states_kernel(k_ref, x_ref, w_ref, out_ref):
-    slabs, rows, size = k_ref.shape
+    )(qkv, keys)
+
+
+def grams_kernel(k_ref, out_ref, *, rows):
+    slabs, _, size = k_ref.shape
     state = jnp.zeros((size, size), jnp.float32)
     for j in range(slabs):
         out_ref[j] = state.astype(out_ref.dtype)
-        if j == slabs - 1:
-            break
-        weighted = jnp.transpose(k_ref[j].astype(jnp.float32)) * w_ref[j, 0:1, :]
-        x = x_ref[j]
-        fresh = dot_nn(split_cat(weighted, 1), jnp.concatenate([x, x], axis=0))
-        state = w_ref[j, 1:2, :size] * state + fresh
-
-
-def states(keys, others, weights):
-    slabs, rows, size = keys.shape
+        if j < slabs - 1:
+            decay, fresh = fresh_state(k_ref[j], k_ref[j, :rows, :])
+            state = decay * state + fresh
+
+
+def grams(keys, rows):
+    slabs, _, size = keys.shape
     return pl.pallas_call(
-        states_kernel,
+        functools.partial(grams_kernel, rows=rows),
         out_shape=jax.ShapeDtypeStruct((slabs, size, size), jnp.bfloat16),
-        name="states",
-    )(keys, others, weights)
+        name="grams",
+    )(keys)
 
 
 def solve_kernel(q_ref, k_ref, rate_ref, gate_ref, ridge_ref, gram_ref, x_ref, p_ref):
@@ -317,18 +390,18 @@
     )(queries, keys, packed(rates), packed(gates), packed(ridge), gram)
 
 
-def finish_kernel(x_ref, p_ref, v_ref, cross_ref, att_ref, out_ref):
+def finish_kernel(x_ref, p_ref, back_ref, att_ref, out_ref):
     heads, rows, size = x_ref.shape
     for h in range(heads):
         cols = slice(h * size, (h + 1) * size)
-        value = v_ref[h]
+        value = back_ref[h, :rows, :]
         att_ref[:, cols] = value
-        out_ref[:, cols] = (dot_nn(x_ref[h], cross_ref[h]) + dot_nn(p_ref[h], value)).astype(
+        out_ref[:, cols] = (dot_nn(x_ref[h], back_ref[h, rows:, :]) + dot_nn(p_ref[h], value)).astype(
             out_ref.dtype
         )
 
 
-def finish(x, products, values, cross, group):
+def finish(x, products, back, group):
     heads, rows, size = x.shape
 
     def spec(a):
@@ -339,11 +412,11 @@
     return pl.pallas_call(
         finish_kernel,
         grid=(heads // group,),
-        in_specs=[spec(x), spec(products), spec(values), spec(cross)],
+        in_specs=[spec(x), spec(products), spec(back)],
         out_specs=[flat, flat],
         out_shape=[shape, shape],
         name="finish",
-    )(x, products, values, cross)
+    )(x, products, back)
 
 
 def exchange(value):
@@ -360,25 +433,16 @@
 ):
     rows = attn_query.shape[0]
     heads, size = regularizer.shape
-    lower = jnp.tril(jnp.ones((rows, rows), jnp.float32))
-    rates = jnp.einsum("th,st->hs", log_decay, lower, precision=exact_mode)
-    gates = jnp.transpose(input_gate)
-    last = rates[:, -1:]
-    weights = jnp.stack(
-        [jnp.exp(last - rates) * gates, jnp.broadcast_to(jnp.exp(last), rates.shape)], axis=1
-    )
+    packed, rates, gates = pack_keys(mesa_key, log_decay, input_gate, size)
+    keys = exchange(packed)
     qkv = exchange(
         jnp.concatenate([by_head(a, heads) for a in (attn_query, attn_key, attn_value)], axis=1)
     )
-    weights = exchange(weights)
-    keys = exchange(by_head(mesa_key, heads))
-    gram = exchange(states(keys, keys, weights))
-    values = attend(qkv, rows, WINDOW // rows)
-    local_values = exchange(values)
-    cross = exchange(states(keys, values, weights))
+    gram = exchange(grams(keys, rows))
+    back = exchange(attend(qkv, keys, rows, WINDOW // rows))
     group = 2 if heads % 2 == 0 else 1
     x, products = solve(mesa_query, mesa_key, rates, gates, regularizer, gram, group)
-    return tuple(finish(x, products, local_values, cross, group))
+    return tuple(finish(x, products, back, group))
 
 
 def body(

time: 221 us -> 196 us (0.89)
  blocking collectives: 18.8 us -> 0 us
  starting transfers between devices: 30.9 us -> 23.8 us
    all_to_all x1 -> x0, blocking collectives: 18.8 us -> none  [exchange(): return lax.all_to_all(value, 'seq', 0, 0, tiled=True)]
    all_to_all x5 -> x4, starting transfers between devices: 30.9 us -> 23.8 us  [exchange(): return lax.all_to_all(value, 'seq', 0, 0, tiled=True)]
    all_to_all x5 -> x4, waiting for transfers between devices: 79.9 us -> 81.6 us  [exchange(): return lax.all_to_all(value, 'seq', 0, 0, tiled=True)]
    reshape x4 -> x3, local copies, waits for them, and re-layouts: 4.59 us -> 3.28 us  [by_head(): return jnp.transpose(value.reshape(rows, heads, -1), (1, 0, 2))]
    unnamed x18 -> x17, local copies, waits for them, and re-layouts: 7.74 us -> 8.71 us
  transfers between devices with their start and end apart: 5 -> 4, of which waited for: 2 -> 2; matrix products, arithmetic and copies ran while one was open for 6% -> 6% of each run, Pallas kernels for 29% -> 32%
where the time goes in v2:
time: 196 us; the launch traced here: 194 us
  waiting for transfers between devices  81.6 us (42%)
  Pallas kernels  71.5 us (36%)
  starting transfers between devices  23.8 us (12%)
  local copies, waits for them, and re-layouts  13.2 us (7%)
  other arithmetic  2.95 us (2%)
    all_to_all x4, waiting for transfers between devices, exchange(): return lax.all_to_all(value, 'seq', 0, 0, tiled=True)  81.6 us
    pallas_call x1, Pallas kernels, solve(): pl.pallas_call(solve_kernel, grid=(steps,), in_specs=[wide, wide, small(r...  36.3 us
    all_to_all x4, starting transfers between devices, exchange(): return lax.all_to_all(value, 'seq', 0, 0, tiled=True)  23.8 us
    pallas_call x1, Pallas kernels, attend(): pl.pallas_call(functools.partial(attend_kernel, rows=rows, reach=reach),...  22.5 us
    unnamed x17, local copies, waits for them, and re-layouts  8.71 us
    pallas_call x1, Pallas kernels, finish(): pl.pallas_call(finish_kernel, grid=(heads // group,), in_specs=[spec(x),...  6.86 us
  transfers between devices with their start and end apart: 4, of which 2 were waited for; matrix products, arithmetic and copies ran while one was open for 6% of the time, Pallas kernels for 32%

profile of v2, /device:TPU:29, one launch (start us, length us, event | category | flops | bytes accessed | tf_op | source)
XLA Modules:
  0.0 193.9 jit_solution(1297733526606671683)
XLA Ops:
  0.6 1.6 copy.12.rate_ref
  2.2 1.5 copy.13.gate_ref
  3.7 3.0 %pack_keys.1 = (bf16[16,272,128]{2,1,0:T(8,128)(2,1)}, f32[16,256]{1,0:T(8,128)}, f32[16,256]{1,0:T(8,128)}) custom-call(bf16[256,2048]{1,0:T(8,128)(2,1)} %k_ref.3, f32[256,16]{1,0:T(8,128)} %copy.12.rate_ref, f32[256,16]{1,0:T(8,128)} %copy.13.gate_ref), custom_call_target="tpu_custom_call" | custom-call | tf_op jit(solution)/shard_map/pack_keys/pallas_call | solution.py:213
  6.6 6.3 %all-to-all-start = ((bf16[16,272,128]{2,1,0:T(8,128)(2,1)}), bf16[16,272,128]{2,1,0:T(8,128)(2,1)S(1)}, u32[]{:S(2)}, u32[]{:S(2)}) async-start(bf16[16,272,128]{2,1,0:T(8,128)(2,1)} %get-tuple-element.9), calls=%async_computation | async-start | bytes 2228224 | tf_op jit(solution)/shard_map/all_to_all | solution.py:423
  12.9 0.5 copy.14
  13.5 0.7 copy.15
  14.1 1.5 copy.16
  15.6 1.3 copy.17
  16.9 1.5 copy.18
  18.4 1.3 copy.19
  19.7 2.9 %pad_maximum_fusion = bf16[16,768,128]{2,1,0:T(8,128)(2,1)} fusion(bf16[16,256,128]{2,1,0:T(8,128)(2,1)} %bitcast.12, bf16[16,256,128]{2,1,0:T(8,128)(2,1)} %bitcast.11, bf16[16,256,128]{2,1,0:T(8,128)(2,1)S(1)} %bitcast.10), kind=kLoop, calls=%fused_computation | loop fusion | flops 9437184 | bytes 6291456 | tf_op jit(solution)/shard_map/concatenate | solution.py:439
  22.7 15.6 %all-to-all-done.k_ref.key_ref = bf16[16,272,128]{2,1,0:T(8,128)(2,1)S(1)} async-done(((bf16[16,272,128]{2,1,0:T(8,128)(2,1)}), bf16[16,272,128]{2,1,0:T(8,128)(2,1)S(1)}, u32[]{:S(2)}, u32[]{:S(2)}) %all-to-all-start) | async-done | bytes 1114144 | tf_op jit(solution)/shard_map/all_to_all | solution.py:423
  38.3 1.0 copy-done.1
  39.3 5.7 %all-to-all-start.2 = ((bf16[16,768,128]{2,1,0:T(8,128)(2,1)}), bf16[16,768,128]{2,1,0:T(8,128)(2,1)S(1)}, u32[]{:S(2)}, u32[]{:S(2)}) async-start(bf16[16,768,128]{2,1,0:T(8,128)(2,1)} %pad_maximum_fusion), calls=%async_computation.2 | async-start | bytes 6291456 | tf_op jit(solution)/shard_map/all_to_all | solution.py:423
  45.1 2.9 %grams.1 = bf16[16,128,128]{2,1,0:T(8,128)(2,1)} custom-call(bf16[16,272,128]{2,1,0:T(8,128)(2,1)} %copy-done.1), custom_call_target="tpu_custom_call" | custom-call | tf_op jit(solution)/shard_map/grams/pallas_call | solution.py:300
  47.9 66.0 %all-to-all-done.2.qkv_ref = bf16[16,768,128]{2,1,0:T(8,128)(2,1)S(1)} async-done(((bf16[16,768,128]{2,1,0:T(8,128)(2,1)}), bf16[16,768,128]{2,1,0:T(8,128)(2,1)S(1)}, u32[]{:S(2)}, u32[]{:S(2)}) %all-to-all-start.2) | async-done | bytes 3145760 | tf_op jit(solution)/shard_map/all_to_all | solution.py:423
  114.0 5.7 %all-to-all-start.1 = ((bf16[16,128,128]{2,1,0:T(8,128)(2,1)}), bf16[16,128,128]{2,1,0:T(8,128)(2,1)}, u32[]{:S(2)}, u32[]{:S(2)}) async-start(bf16[16,128,128]{2,1,0:T(8,128)(2,1)} %grams.1), calls=%async_computation.1 | async-start | bytes 1048576 | tf_op jit(solution)/shard_map/all_to_all | solution.py:423
  119.7 22.5 %attend.1 = bf16[16,384,128]{2,1,0:T(8,128)(2,1)} custom-call(bf16[16,768,128]{2,1,0:T(8,128)(2,1)} %copy-done, bf16[16,272,128]{2,1,0:T(8,128)(2,1)} %copy-done.1), custom_call_target="tpu_custom_call" | custom-call | tf_op jit(solution)/shard_map/attend/pallas_call | solution.py:274
  142.3 6.0 %all-to-all-start.3 = ((bf16[16,384,128]{2,1,0:T(8,128)(2,1)}), bf16[16,384,128]{2,1,0:T(8,128)(2,1)S(1)}, u32[]{:S(2)}, u32[]{:S(2)}) async-start(bf16[16,384,128]{2,1,0:T(8,128)(2,1)} %attend.1), calls=%async_computation.3 | async-start | bytes 3145728 | tf_op jit(solution)/shard_map/all_to_all | solution.py:423
  148.3 0.6 reshape.22.rate_ref
  148.9 0.6 reshape.23.gate_ref
  149.5 36.3 %solve.1 = (bf16[16,256,128]{2,1,0:T(8,128)(2,1)}, bf16[16,256,256]{2,1,0:T(8,128)(2,1)}) custom-call(bf16[256,2048]{1,0:T(8,128)(2,1)} %q_ref.1, bf16[256,2048]{1,0:T(8,128)(2,1)} %k_ref.3, f32[8,2,256]{2,1,0:T(2,128)} %reshape.22.rate_ref, f32[8,2,256]{2,1,0:T(2,128)} %reshape.23.gate_ref, f32[8,2,128]{2,1,0:T(2,128)} %bitcast.13, ...), custom_call_target="tpu_custom_call" | custom-call | tf_op jit(solution)/shard_map/solve/pallas_call | solution.py:370
  185.9 1.2 copy-done.2
  187.0 6.9 %finish.1 = (bf16[256,2048]{1,0:T(8,128)(2,1)}, bf16[256,2048]{1,0:T(8,128)(2,1)}) custom-call(bf16[16,256,128]{2,1,0:T(8,128)(2,1)} %get-tuple-element.10.x_ref, bf16[16,256,256]{2,1,0:T(8,128)(2,1)} %get-tuple-element.11.p_ref, bf16[16,384,128]{2,1,0:T(8,128)(2,1)} %copy-done.2), custom_call_target="tpu_custom_call" | custom-call | tf_op jit(solution)/shard_map/finish/pallas_call | solution.py:412
  (12 shorter events, 0.0 us)
Async XLA Ops:
  0.6 12.3 %copy-start.3 = (bf16[256,2048]{1,0:T(8,128)(2,1)S(1)}, bf16[256,2048]{1,0:T(8,128)(2,1)}, u32[]{:S(2)}) copy-start(bf16[256,2048]{1,0:T(8,128)(2,1)} %param.8) | copy-start | bytes 3145732
  6.6 31.6 %all-to-all-start = ((bf16[16,272,128]{2,1,0:T(8,128)(2,1)}), bf16[16,272,128]{2,1,0:T(8,128)(2,1)S(1)}, u32[]{:S(2)}, u32[]{:S(2)}) async-start(bf16[16,272,128]{2,1,0:T(8,128)(2,1)} %get-tuple-element.9), calls=%async_computation | async-start | bytes 2228224 | tf_op jit(solution)/shard_map/all_to_all | solution.py:423
  38.3 1.0 copy-start.1
  39.3 74.7 %all-to-all-start.2 = ((bf16[16,768,128]{2,1,0:T(8,128)(2,1)}), bf16[16,768,128]{2,1,0:T(8,128)(2,1)S(1)}, u32[]{:S(2)}, u32[]{:S(2)}) async-start(bf16[16,768,128]{2,1,0:T(8,128)(2,1)} %pad_maximum_fusion), calls=%async_computation.2 | async-start | bytes 6291456 | tf_op jit(solution)/shard_map/all_to_all | solution.py:423
  114.0 5.7 %copy-start = (bf16[16,768,128]{2,1,0:T(8,128)(2,1)}, bf16[16,768,128]{2,1,0:T(8,128)(2,1)S(1)}, u32[]{:S(2)}) copy-start(bf16[16,768,128]{2,1,0:T(8,128)(2,1)S(1)} %all-to-all-done.2.qkv_ref) | copy-start | bytes 9437188
  114.0 28.3 %all-to-all-start.1 = ((bf16[16,128,128]{2,1,0:T(8,128)(2,1)}), bf16[16,128,128]{2,1,0:T(8,128)(2,1)}, u32[]{:S(2)}, u32[]{:S(2)}) async-start(bf16[16,128,128]{2,1,0:T(8,128)(2,1)} %grams.1), calls=%async_computation.1 | async-start | bytes 1048576 | tf_op jit(solution)/shard_map/all_to_all | solution.py:423
  119.7 28.6 %copy-start.5 = (f32[16,256]{1,0:T(8,128)S(1)}, f32[16,256]{1,0:T(8,128)}, u32[]{:S(2)}) copy-start(f32[16,256]{1,0:T(8,128)} %get-tuple-element.7) | copy-start | bytes 49156
  119.7 29.2 %copy-start.4 = (f32[16,256]{1,0:T(8,128)S(1)}, f32[16,256]{1,0:T(8,128)}, u32[]{:S(2)}) copy-start(f32[16,256]{1,0:T(8,128)} %get-tuple-element.8) | copy-start | bytes 49156
  142.3 43.6 %all-to-all-start.3 = ((bf16[16,384,128]{2,1,0:T(8,128)(2,1)}), bf16[16,384,128]{2,1,0:T(8,128)(2,1)S(1)}, u32[]{:S(2)}, u32[]{:S(2)}) async-start(bf16[16,384,128]{2,1,0:T(8,128)(2,1)} %attend.1), calls=%async_computation.3 | async-start | bytes 3145728 | tf_op jit(solution)/shard_map/all_to_all | solution.py:423
  185.9 1.2 copy-start.2

commit v3 on v2

--- a/solution.py
+++ b/solution.py
@@ -170,24 +170,21 @@
     return decay, dot_nn(weighted, jnp.concatenate([others, others], axis=0))
 
 
-def pack_keys_kernel(k_ref, rate_ref, gate_ref, out_ref, total_ref, gate_out_ref):
+def pack_keys_kernel(k_ref, rate_ref, gate_ref, out_ref, total_ref):
     heads, height, size = out_ref.shape
     rows = k_ref.shape[0]
     count = rows // size
     at = lax.broadcasted_iota(jnp.int32, (rows, rows), 0)
-    lower = (at >= lax.broadcasted_iota(jnp.int32, (rows, rows), 1)).astype(jnp.float32)
-    totals = jnp.transpose(
-        lax.dot_general(
-            lower,
-            rate_ref[...],
-            (((1,), (0,)), ((), ())),
-            precision=exact_mode,
-            preferred_element_type=jnp.float32,
-        )
-    )
-    gates = jnp.transpose(gate_ref[...])
+    upper = (at <= lax.broadcasted_iota(jnp.int32, (rows, rows), 1)).astype(jnp.float32)
+    totals = lax.dot_general(
+        rate_ref[...],
+        upper,
+        (((1,), (0,)), ((), ())),
+        precision=exact_mode,
+        preferred_element_type=jnp.float32,
+    )
+    gates = gate_ref[...]
     total_ref[...] = totals
-    gate_out_ref[...] = gates
     last = totals[:, rows - 1 :]
     weights = jnp.exp(last - totals) * gates
     decays = jnp.broadcast_to(jnp.exp(last), (heads, size))
@@ -214,7 +211,6 @@
         pack_keys_kernel,
         out_shape=[
             jax.ShapeDtypeStruct((heads, rows + spare, size), jnp.bfloat16),
-            small,
             small,
         ],
         name="pack_keys",
@@ -433,16 +429,17 @@
 ):
     rows = attn_query.shape[0]
     heads, size = regularizer.shape
-    packed, rates, gates = pack_keys(mesa_key, log_decay, input_gate, size)
+    gates = jnp.transpose(input_gate)
+    packed, rates = pack_keys(mesa_key, jnp.transpose(log_decay), gates, size)
     keys = exchange(packed)
     qkv = exchange(
         jnp.concatenate([by_head(a, heads) for a in (attn_query, attn_key, attn_value)], axis=1)
     )
     gram = exchange(grams(keys, rows))
     back = exchange(attend(qkv, keys, rows, WINDOW // rows))
-    group = 2 if heads % 2 == 0 else 1
+    group = math.gcd(heads, 4)
     x, products = solve(mesa_query, mesa_key, rates, gates, regularizer, gram, group)
-    return tuple(finish(x, products, back, group))
+    return tuple(finish(x, products, back, math.gcd(heads, 8)))
 
 
 def body(

time: 196 us -> 187 us (0.954)
  Pallas kernels: 71.5 us -> 63.5 us
  local copies, waits for them, and re-layouts: 13.2 us -> 10.2 us
  waiting for transfers between devices: 81.6 us -> 84 us
    pallas_call x1, Pallas kernels: 36.3 us -> 31.6 us  [solve(): pl.pallas_call(solve_kernel, grid=(steps,), in_specs=[wide, wide, small(r...]
    pallas_call x1, Pallas kernels: 6.86 us -> 3.69 us  [finish(): pl.pallas_call(finish_kernel, grid=(heads // group,), in_specs=[spec(x),...]
    unnamed x17 -> x15, local copies, waits for them, and re-layouts: 8.71 us -> 5.69 us
    all_to_all x4, waiting for transfers between devices: 81.6 us -> 84 us  [exchange(): return lax.all_to_all(value, 'seq', 0, 0, tiled=True)]
  transfers between devices with their start and end apart: 4 -> 4, of which waited for: 2 -> 3; matrix products, arithmetic and copies ran while one was open for 6% -> 6% of each run, Pallas kernels for 32% -> 31%
where the time goes in v3:
time: 187 us; the launch traced here: 185 us
  waiting for transfers between devices  84 us (45%)
  Pallas kernels  63.5 us (34%)
  starting transfers between devices  23.8 us (13%)
  local copies, waits for them, and re-layouts  10.2 us (5%)
  other arithmetic  2.95 us (2%)
    all_to_all x4, waiting for transfers between devices, exchange(): return lax.all_to_all(value, 'seq', 0, 0, tiled=True)  84 us
    pallas_call x1, Pallas kernels, solve(): pl.pallas_call(solve_kernel, grid=(steps,), in_specs=[wide, wide, small(r...  31.6 us
    all_to_all x4, starting transfers between devices, exchange(): return lax.all_to_all(value, 'seq', 0, 0, tiled=True)  23.8 us
    pallas_call x1, Pallas kernels, attend(): pl.pallas_call(functools.partial(attend_kernel, rows=rows, reach=reach),...  22.5 us
    unnamed x15, local copies, waits for them, and re-layouts  5.69 us
  transfers between devices with their start and end apart: 4, of which 3 were waited for; matrix products, arithmetic and copies ran while one was open for 6% of the time, Pallas kernels for 31%

profile of v3, /device:TPU:29, one launch (start us, length us, event | category | flops | bytes accessed | tf_op | source)
XLA Modules:
  0.0 185.2 jit_solution(4648406965591275133)
XLA Ops:
  0.6 2.8 %pack_keys.1 = (bf16[16,272,128]{2,1,0:T(8,128)(2,1)}, f32[16,256]{1,0:T(8,128)}) custom-call(bf16[256,2048]{1,0:T(8,128)(2,1)} %k_ref.3, f32[16,256]{1,0:T(8,128)} %bitcast.17, f32[16,256]{1,0:T(8,128)} %bitcast.15), custom_call_target="tpu_custom_call" | custom-call | tf_op jit(solution)/shard_map/pack_keys/pallas_call | solution.py:210
  3.4 6.3 %all-to-all-start = ((bf16[16,272,128]{2,1,0:T(8,128)(2,1)}), bf16[16,272,128]{2,1,0:T(8,128)(2,1)S(1)}, u32[]{:S(2)}, u32[]{:S(2)}) async-start(bf16[16,272,128]{2,1,0:T(8,128)(2,1)} %get-tuple-element.7), calls=%async_computation | async-start | bytes 2228224 | tf_op jit(solution)/shard_map/all_to_all | solution.py:419
  9.7 0.5 copy.10
  10.3 0.7 copy.11
  10.9 1.5 copy.12
  12.4 1.3 copy.13
  13.7 1.5 copy.14
  15.2 1.3 copy.15
  16.5 2.9 %pad_maximum_fusion = bf16[16,768,128]{2,1,0:T(8,128)(2,1)} fusion(bf16[16,256,128]{2,1,0:T(8,128)(2,1)} %bitcast.14, bf16[16,256,128]{2,1,0:T(8,128)(2,1)} %bitcast.13, bf16[16,256,128]{2,1,0:T(8,128)(2,1)S(1)} %bitcast.12), kind=kLoop, calls=%fused_computation | loop fusion | flops 9437184 | bytes 6291456 | tf_op jit(solution)/shard_map/concatenate | solution.py:436
  19.5 15.6 %all-to-all-done.k_ref.key_ref = bf16[16,272,128]{2,1,0:T(8,128)(2,1)S(1)} async-done(((bf16[16,272,128]{2,1,0:T(8,128)(2,1)}), bf16[16,272,128]{2,1,0:T(8,128)(2,1)S(1)}, u32[]{:S(2)}, u32[]{:S(2)}) %all-to-all-start) | async-done | bytes 1114144 | tf_op jit(solution)/shard_map/all_to_all | solution.py:419
  35.1 1.0 copy-done.1
  36.1 5.7 %all-to-all-start.2 = ((bf16[16,768,128]{2,1,0:T(8,128)(2,1)}), bf16[16,768,128]{2,1,0:T(8,128)(2,1)S(1)}, u32[]{:S(2)}, u32[]{:S(2)}) async-start(bf16[16,768,128]{2,1,0:T(8,128)(2,1)} %pad_maximum_fusion), calls=%async_computation.2 | async-start | bytes 6291456 | tf_op jit(solution)/shard_map/all_to_all | solution.py:419
  41.8 2.9 %grams.1 = bf16[16,128,128]{2,1,0:T(8,128)(2,1)} custom-call(bf16[16,272,128]{2,1,0:T(8,128)(2,1)} %copy-done.1), custom_call_target="tpu_custom_call" | custom-call | tf_op jit(solution)/shard_map/grams/pallas_call | solution.py:296
  44.7 66.0 %all-to-all-done.2.qkv_ref = bf16[16,768,128]{2,1,0:T(8,128)(2,1)S(1)} async-done(((bf16[16,768,128]{2,1,0:T(8,128)(2,1)}), bf16[16,768,128]{2,1,0:T(8,128)(2,1)S(1)}, u32[]{:S(2)}, u32[]{:S(2)}) %all-to-all-start.2) | async-done | bytes 3145760 | tf_op jit(solution)/shard_map/all_to_all | solution.py:419
  110.8 5.7 %all-to-all-start.1 = ((bf16[16,128,128]{2,1,0:T(8,128)(2,1)}), bf16[16,128,128]{2,1,0:T(8,128)(2,1)}, u32[]{:S(2)}, u32[]{:S(2)}) async-start(bf16[16,128,128]{2,1,0:T(8,128)(2,1)} %grams.1), calls=%async_computation.1 | async-start | bytes 1048576 | tf_op jit(solution)/shard_map/all_to_all | solution.py:419
  116.5 0.0 copy-start.4
  116.5 22.5 %attend.1 = bf16[16,384,128]{2,1,0:T(8,128)(2,1)} custom-call(bf16[16,768,128]{2,1,0:T(8,128)(2,1)} %copy-done, bf16[16,272,128]{2,1,0:T(8,128)(2,1)} %copy-done.1), custom_call_target="tpu_custom_call" | custom-call | tf_op jit(solution)/shard_map/attend/pallas_call | solution.py:270
  139.1 6.0 %all-to-all-start.3 = ((bf16[16,384,128]{2,1,0:T(8,128)(2,1)}), bf16[16,384,128]{2,1,0:T(8,128)(2,1)S(1)}, u32[]{:S(2)}, u32[]{:S(2)}) async-start(bf16[16,384,128]{2,1,0:T(8,128)(2,1)} %attend.1), calls=%async_computation.3 | async-start | bytes 3145728 | tf_op jit(solution)/shard_map/all_to_all | solution.py:419
  145.1 0.6 reshape.23.gate_ref
  145.7 0.6 reshape.22.rate_ref
  146.3 31.6 %solve.1 = (bf16[16,256,128]{2,1,0:T(8,128)(2,1)}, bf16[16,256,256]{2,1,0:T(8,128)(2,1)}) custom-call(bf16[256,2048]{1,0:T(8,128)(2,1)} %q_ref.1, bf16[256,2048]{1,0:T(8,128)(2,1)} %k_ref.3, f32[4,4,256]{2,1,0:T(4,128)} %reshape.22.rate_ref, f32[4,4,256]{2,1,0:T(4,128)} %reshape.23.gate_ref, f32[4,4,128]{2,1,0:T(4,128)} %bitcast.18, ...), custom_call_target="tpu_custom_call" | custom-call | tf_op jit(solution)/shard_map/solve/pallas_call | solution.py:366
  178.0 2.4 %all-to-all-done.3.back_ref = bf16[16,384,128]{2,1,0:T(8,128)(2,1)S(1)} async-done(((bf16[16,384,128]{2,1,0:T(8,128)(2,1)}), bf16[16,384,128]{2,1,0:T(8,128)(2,1)S(1)}, u32[]{:S(2)}, u32[]{:S(2)}) %all-to-all-start.3) | async-done | bytes 1572896 | tf_op jit(solution)/shard_map/all_to_all | solution.py:419
  180.3 1.2 copy-done.2
  181.5 3.7 %finish.1 = (bf16[256,2048]{1,0:T(8,128)(2,1)}, bf16[256,2048]{1,0:T(8,128)(2,1)}) custom-call(bf16[16,256,128]{2,1,0:T(8,128)(2,1)} %get-tuple-element.8.x_ref, bf16[16,256,256]{2,1,0:T(8,128)(2,1)} %get-tuple-element.9.p_ref, bf16[16,384,128]{2,1,0:T(8,128)(2,1)} %copy-done.2), custom_call_target="tpu_custom_call" | custom-call | tf_op jit(solution)/shard_map/finish/pallas_call | solution.py:408
  (10 shorter events, 0.0 us)
Async XLA Ops:
  0.6 9.1 %copy-start.3 = (bf16[256,2048]{1,0:T(8,128)(2,1)S(1)}, bf16[256,2048]{1,0:T(8,128)(2,1)}, u32[]{:S(2)}) copy-start(bf16[256,2048]{1,0:T(8,128)(2,1)} %param.8) | copy-start | bytes 3145732
  3.4 31.6 %all-to-all-start = ((bf16[16,272,128]{2,1,0:T(8,128)(2,1)}), bf16[16,272,128]{2,1,0:T(8,128)(2,1)S(1)}, u32[]{:S(2)}, u32[]{:S(2)}) async-start(bf16[16,272,128]{2,1,0:T(8,128)(2,1)} %get-tuple-element.7), calls=%async_computation | async-start | bytes 2228224 | tf_op jit(solution)/shard_map/all_to_all | solution.py:419
  35.1 1.0 copy-start.1
  36.1 74.7 %all-to-all-start.2 = ((bf16[16,768,128]{2,1,0:T(8,128)(2,1)}), bf16[16,768,128]{2,1,0:T(8,128)(2,1)S(1)}, u32[]{:S(2)}, u32[]{:S(2)}) async-start(bf16[16,768,128]{2,1,0:T(8,128)(2,1)} %pad_maximum_fusion), calls=%async_computation.2 | async-start | bytes 6291456 | tf_op jit(solution)/shard_map/all_to_all | solution.py:419
  110.8 5.7 %copy-start = (bf16[16,768,128]{2,1,0:T(8,128)(2,1)}, bf16[16,768,128]{2,1,0:T(8,128)(2,1)S(1)}, u32[]{:S(2)}) copy-start(bf16[16,768,128]{2,1,0:T(8,128)(2,1)S(1)} %all-to-all-done.2.qkv_ref) | copy-start | bytes 9437188
  110.8 28.3 %all-to-all-start.1 = ((bf16[16,128,128]{2,1,0:T(8,128)(2,1)}), bf16[16,128,128]{2,1,0:T(8,128)(2,1)}, u32[]{:S(2)}, u32[]{:S(2)}) async-start(bf16[16,128,128]{2,1,0:T(8,128)(2,1)} %grams.1), calls=%async_computation.1 | async-start | bytes 1048576 | tf_op jit(solution)/shard_map/all_to_all | solution.py:419
  116.5 28.6 %copy-start.4 = (f32[256,16]{0,1:T(8,128)S(1)}, f32[256,16]{0,1:T(8,128)}, u32[]{:S(2)}) copy-start(f32[256,16]{0,1:T(8,128)} %param.14) | copy-start | bytes 49156
  116.5 29.2 %copy-start.5 = (f32[16,256]{1,0:T(8,128)S(1)}, f32[16,256]{1,0:T(8,128)}, u32[]{:S(2)}) copy-start(f32[16,256]{1,0:T(8,128)} %get-tuple-element.6) | copy-start | bytes 49156
  139.1 41.3 %all-to-all-start.3 = ((bf16[16,384,128]{2,1,0:T(8,128)(2,1)}), bf16[16,384,128]{2,1,0:T(8,128)(2,1)S(1)}, u32[]{:S(2)}, u32[]{:S(2)}) async-start(bf16[16,384,128]{2,1,0:T(8,128)(2,1)} %attend.1), calls=%async_computation.3 | async-start | bytes 3145728 | tf_op jit(solution)/shard_map/all_to_all | solution.py:419
  180.3 1.2 copy-start.2
